TPU v7x, 32 devices: a whole 2x2x4 slice. The times are simulated.
32 devices in a mesh: row: 8 (over y, x, core), col: 4 (over z).
Axes of the slice: x: 2, y: 2, z: 4, core: 2. Of those that a mesh axis runs over, the one named last changes fastest.
Arguments:
- surface_height: float32 [2048, 2048], P('row', 'col'), may hold values from -1.2 to 1.2
- surface_potential: float32 [2048, 2048], P('row', 'col'), may hold values from -4 to 4
- velocity: float32 [3, 16, 1024, 1024], P(None, None, 'row', 'col'), may hold values from -1.25 to 1.25
Outputs:
- height_rate: float32 [2048, 2048], P('row', 'col')
- potential_rate: float32 [2048, 2048], P('row', 'col')
- velocity_next: float32 [3, 16, 1024, 1024], P(None, None, 'row', 'col')
All inputs are finite; a program needn't handle non-finite values.
Results may differ from a plain program's by a relative error of at most 0.00019.
Values sent between devices are 32-bit elements; how exact they have to be, the bound alone decides.
No kernel may reach another device: no remote copies, remote signals or barrier semaphores. Data moves between devices by JAX's collectives and lax.ppermute only.
A program may use at most 192 MiB of HBM per device.

v0:
```python
import jax
import jax.numpy as jnp
from jax import lax
from jax.sharding import PartitionSpec as P

NX = 2048
NY = 2048
COARSE = 2
GRAVITY = 1.0
SURFACE_STEP = 0.05
FLOW_STEP = 0.5
VISCOSITY = 0.2
DECAY_RATE = 0.05


def with_halo(x, sides, width):
    for axis, dim in sides:
        peers, length = (lax.axis_size(axis), x.shape[dim])
        up = [(i, (i + 1) % peers) for i in range(peers)]
        down = [(j, i) for i, j in up]
        last = lax.slice_in_dim(x, length - width, length, axis=dim)
        leading = lax.slice_in_dim(x, 0, width, axis=dim)
        before = lax.ppermute(last, axis, up)
        after = lax.ppermute(leading, axis, down)
        x = jnp.concatenate([before, x, after], axis=dim)
    return x


def wave_numbers(index, length):
    signed = jnp.where(index < length // 2, index, index - length)
    kept_mask = (jnp.abs(signed) <= length // 3).astype(jnp.float32)
    return (2.0 * jnp.pi / length * signed.astype(jnp.float32), kept_mask)


def coarsen(source):
    rows_out = source.shape[0] // COARSE
    cols_out = source.shape[1] // COARSE
    return source.reshape(rows_out, COARSE, cols_out, COARSE).mean(axis=(1, 3))


def flow_update(padded_flow, padded_load, surface_u, surface_v):
    depth_count = padded_flow.shape[1]
    level_mid = jnp.arange(depth_count, dtype=jnp.float32)[:, None, None] + 0.5
    drift_decay = jnp.exp(-2.0 * DECAY_RATE * level_mid)
    load_decay = jnp.exp(-DECAY_RATE * level_mid)

    def derivs(source, top_value):
        middle = source[:, 1:-1, 1:-1]
        above_cell = jnp.concatenate([top_value[None], middle[:-1]], axis=0)
        below_cell = jnp.concatenate([middle[1:], middle[-1:]], axis=0)
        east_side = source[:, 1:-1, 2:]
        west_side = source[:, 1:-1, :-2]
        north_side = source[:, 2:, 1:-1]
        south_side = source[:, :-2, 1:-1]
        laplace = (
            east_side + west_side + north_side + south_side + above_cell + below_cell - 6.0 * middle
        )
        return (
            middle,
            0.5 * (east_side - west_side),
            0.5 * (north_side - south_side),
            0.5 * (above_cell - below_cell),
            laplace,
        )

    u_mid, u_dx, u_dy, u_dz, u_lap = derivs(padded_flow[0], surface_u)
    v_mid, v_dx, v_dy, v_dz, v_lap = derivs(padded_flow[1], surface_v)
    w_mid, w_dx, w_dy, w_dz, w_lap = derivs(padded_flow[2], jnp.zeros_like(surface_u))
    vort_x = w_dy - v_dz
    vort_y = u_dz - w_dx
    vort_z = v_dx - u_dy
    drift_u = surface_u[None] * drift_decay
    drift_v = surface_v[None] * drift_decay
    load_x = 0.5 * (padded_load[1:-1, 2:] - padded_load[1:-1, :-2])[None] * load_decay
    load_y = 0.5 * (padded_load[2:, 1:-1] - padded_load[:-2, 1:-1])[None] * load_decay

    def advance(middle, slope_x, slope_y, slope_z, laplace, forcing):
        carried = u_mid * slope_x + v_mid * slope_y + w_mid * slope_z
        return middle + FLOW_STEP * (-carried + VISCOSITY * laplace + forcing)

    next_u = advance(u_mid, u_dx, u_dy, u_dz, u_lap, drift_v * vort_z - load_x)
    next_v = advance(v_mid, v_dx, v_dy, v_dz, v_lap, -drift_u * vort_z - load_y)
    next_w = advance(w_mid, w_dx, w_dy, w_dz, w_lap, drift_u * vort_y - drift_v * vort_x)
    return jnp.stack([next_u, next_v, next_w])


def product(form, left, right):
    return jnp.einsum(form, left, right, precision=lax.Precision.HIGHEST)


def complex_product(form, left_real, left_imag, right_real, right_imag):
    if left_imag is None:
        return (product(form, left_real, right_real), product(form, left_real, right_imag))
    out_real = product(form, left_real, right_real) - product(form, left_imag, right_imag)
    out_imag = product(form, left_real, right_imag) + product(form, left_imag, right_real)
    return (out_real, out_imag)


def tables(length, direction):
    index = jnp.arange(length, dtype=jnp.int32)
    angle = 2.0 * jnp.pi / length * (index[:, None] * index[None, :] % length).astype(jnp.float32)
    return (jnp.cos(angle), direction * jnp.sin(angle))


def twiddles(factor_one, factor_two, direction):
    total = factor_one * factor_two
    index_one = jnp.arange(factor_one, dtype=jnp.int32)
    index_two = jnp.arange(factor_two, dtype=jnp.int32)
    angle = (
        2.0 * jnp.pi / total * (index_one[:, None] * index_two[None, :] % total).astype(jnp.float32)
    )
    return (jnp.cos(angle), direction * jnp.sin(angle))


def transform(real_part, imag_part, direction, layout, real_only):
    if layout == "back":
        length = real_part.shape[1]
    else:
        length = real_part.shape[2]
    factor_one = 1 << (length.bit_length() - 1) // 2
    factor_two = length // factor_one
    cos_one, sin_one = tables(factor_one, direction)
    cos_two, sin_two = tables(factor_two, direction)
    twist_cos, twist_sin = twiddles(factor_one, factor_two, direction)
    batch_size = real_part.shape[0]
    if layout == "back":
        cross_len = real_part.shape[2]
        shape_four = (batch_size, factor_one, factor_two, cross_len)
        first_form = "banm,ak->bknm"
        second_form = "bknm,nq->bmqk"
        twist_cos = twist_cos[None, :, :, None]
        twist_sin = twist_sin[None, :, :, None]
        out_shape = (batch_size, cross_len, length)
    else:
        cross_len = real_part.shape[1]
        shape_four = (batch_size, cross_len, factor_one, factor_two)
        first_form = "bman,ak->bmkn"
        twist_cos = twist_cos[None, None]
        twist_sin = twist_sin[None, None]
        if layout == "front":
            second_form = "bmkn,nq->bqkm"
            out_shape = (batch_size, length, cross_len)
        else:
            second_form = "bmkn,nq->bmqk"
            out_shape = (batch_size, cross_len, length)
    left_real = real_part.reshape(shape_four)
    left_imag = None if imag_part is None else imag_part.reshape(shape_four)
    mid_real, mid_imag = complex_product(first_form, left_real, left_imag, cos_one, sin_one)
    turned_real = mid_real * twist_cos - mid_imag * twist_sin
    turned_imag = mid_real * twist_sin + mid_imag * twist_cos
    if real_only:
        result = product(second_form, turned_real, cos_two) - product(
            second_form, turned_imag, sin_two
        )
        return result.reshape(out_shape)
    out_real, out_imag = complex_product(second_form, turned_real, turned_imag, cos_two, sin_two)
    return (out_real.reshape(out_shape), out_imag.reshape(out_shape))


def scaled(pair_value, factor):
    return (pair_value[0] * factor, pair_value[1] * factor)


def turned(pair_value, factor):
    return (-factor * pair_value[1], factor * pair_value[0])


def unfold_half(full_real, full_imag, kept_modes):
    weights = jnp.where(jnp.arange(kept_modes, dtype=jnp.int32) == 0, 1.0, 2.0).astype(jnp.float32)[
        None, :, None
    ]
    padding = jnp.zeros((full_real.shape[0], NX - kept_modes, full_real.shape[2]), jnp.float32)
    return (
        jnp.concatenate([full_real * weights, padding], axis=1),
        jnp.concatenate([full_imag * weights, padding], axis=1),
    )


def local(surface_height, surface_potential, velocity):
    col_count = lax.axis_size("col")
    device_count = lax.axis_size("row") * col_count
    place = lax.axis_index("row") * col_count + lax.axis_index("col")
    kept_modes = (NX // 3 + device_count) // device_count * device_count
    modes_each = kept_modes // device_count
    kx_index = place * modes_each + jnp.arange(modes_each, dtype=jnp.int32)
    kx_values, kx_kept = wave_numbers(kx_index, NX)
    ky_values, ky_kept = wave_numbers(jnp.arange(NY, dtype=jnp.int32), NY)
    kx_grid = kx_values[:, None]
    ky_grid = ky_values[None, :]
    mask = kx_kept[:, None] * ky_kept[None, :]
    magnitude = jnp.sqrt(kx_grid * kx_grid + ky_grid * ky_grid)

    def forward(stacked):
        pencil = lax.all_to_all(stacked, "col", split_axis=1, concat_axis=2, tiled=True)
        wide_real, wide_imag = transform(pencil, None, -1.0, "front", False)
        slab_real, slab_imag = (
            lax.all_to_all(
                wide_real[:, :kept_modes], ("row", "col"), split_axis=1, concat_axis=2, tiled=True
            ),
            lax.all_to_all(
                wide_imag[:, :kept_modes], ("row", "col"), split_axis=1, concat_axis=2, tiled=True
            ),
        )
        spec_real, spec_imag = transform(slab_real, slab_imag, -1.0, "last", False)
        return (spec_real * mask, spec_imag * mask)

    def inverse(pair_list):
        spec_real = jnp.stack([pair_item[0] for pair_item in pair_list])
        spec_imag = jnp.stack([pair_item[1] for pair_item in pair_list])
        line_real, line_imag = transform(spec_real, spec_imag, 1.0, "last", False)
        full_real, full_imag = (
            lax.all_to_all(line_real, ("row", "col"), split_axis=2, concat_axis=1, tiled=True),
            lax.all_to_all(line_imag, ("row", "col"), split_axis=2, concat_axis=1, tiled=True),
        )
        full_real, full_imag = unfold_half(full_real, full_imag, kept_modes)
        pencil = transform(full_real, full_imag, 1.0, "back", True) / float(NX * NY)
        return lax.all_to_all(pencil, "col", split_axis=2, concat_axis=1, tiled=True)

    first_real, first_imag = forward(jnp.stack([surface_potential, surface_height]))
    pot_hat = (first_real[0], first_imag[0])
    height_hat = (first_real[1], first_imag[1])
    first_fields = inverse(
        [
            scaled(pot_hat, magnitude),
            scaled(pot_hat, magnitude * magnitude),
            scaled(pot_hat, magnitude * magnitude * magnitude),
            turned(pot_hat, kx_grid),
            turned(pot_hat, ky_grid),
            turned(height_hat, kx_grid),
            turned(height_hat, ky_grid),
        ]
    )
    vert_one = first_fields[0]
    curve_one = first_fields[1]
    cube_one = first_fields[2]
    pot_dx = first_fields[3]
    pot_dy = first_fields[4]
    height_dx = first_fields[5]
    height_dy = first_fields[6]
    second_pot = -surface_height * vert_one
    second_real, second_imag = forward(second_pot[None])
    second_hat = (second_real[0], second_imag[0])
    second_fields = inverse(
        [scaled(second_hat, magnitude), scaled(second_hat, magnitude * magnitude)]
    )
    vert_two = second_fields[0]
    curve_two = second_fields[1]
    third_pot = -surface_height * vert_two - 0.5 * surface_height * surface_height * curve_one
    third_real, third_imag = forward(third_pot[None])
    vert_three = inverse([scaled((third_real[0], third_imag[0]), magnitude)])[0]
    vertical = (
        vert_one
        + vert_two
        + vert_three
        + surface_height * (curve_one + curve_two)
        + 0.5 * surface_height * surface_height * cube_one
    )
    slope = height_dx * height_dx + height_dy * height_dy
    height_rate = -(height_dx * pot_dx + height_dy * pot_dy) + (1.0 + slope) * vertical
    potential_rate = (
        -GRAVITY * surface_height
        - 0.5 * (pot_dx * pot_dx + pot_dy * pot_dy)
        + 0.5 * (1.0 + slope) * vertical * vertical
    )
    pressure = GRAVITY * coarsen(surface_height + SURFACE_STEP * height_rate)
    surface_u = coarsen(pot_dx)
    surface_v = coarsen(pot_dy)
    depth_count = velocity.shape[1]
    stacked_block = jnp.concatenate(
        [velocity.reshape((3 * depth_count,) + velocity.shape[2:]), pressure[None]], axis=0
    )
    padded_block = with_halo(stacked_block, (("row", 1), ("col", 2)), 1)
    padded_flow = padded_block[:-1].reshape((3, depth_count) + padded_block.shape[1:])
    padded_load = padded_block[-1]
    velocity_next = flow_update(padded_flow, padded_load, surface_u, surface_v)
    return (height_rate, potential_rate, velocity_next)


def solution(mesh):
    placed = (P("row", "col"), P("row", "col"), P(None, None, "row", "col"))
    return jax.shard_map(
        local,
        mesh=mesh,
        in_specs=placed,
        out_specs=(P("row", "col"), P("row", "col"), P(None, None, "row", "col")),
        check_vma=False,
    )
```

profile of v0, /device:TPU:0, one launch (start us, length us, event | category | flops | bytes accessed | tf_op | source)
XLA Modules:
  0.0 1156.2 jit_solution(16676131962339563223)
XLA Ops:
  12.0 25.5 %all-to-all-done = f32[2,256,512]{2,0,1:T(2,128)S(1)} async-done(((f32[2,256,512]{2,0,1:T(2,128)}), f32[2,256,512]{2,0,1:T(2,128)S(1)}, u32[]{:S(2)}, u32[]{:S(2)}) %all-to-all-start) | async-done | bytes 1048608 | tf_op jit(solution)/shard_map/all_to_all | solution.py:194
  54.0 18.9 %subtract_bitcast_fusion.3 = f32[2,64,32,64]{3,1,2,0:T(8,128)S(1)} fusion(f32[64,2,64,32]{2,0,3,1:T(8,128)S(1)} %fusion.71, f32[2,64,32,64]{3,2,1,0:T(8,128)S(1)} %get-tuple-element.49), kind=kOutput, calls=%fused_computation.117 | convolution fusion | flops 201646080 | bytes 3145728 | tf_op jit(solution)/shard_map/bmkn,nq->bqkm/dot_general | solution.py:88
  294.1 14.8 %fusion.4 = f32[32,7,64,64]{3,0,2,1:T(8,128)} fusion(f32[7,32,64,64]{3,2,1,0:T(8,128)S(1)} %bitcast.784), kind=kOutput, calls=%fused_computation.7 | convolution fusion | flops 352335872 | bytes 7340032 | tf_op jit(solution)/shard_map/banm,ak->bknm/dot_general | solution.py:88
  308.9 14.9 %fusion.6 = f32[32,7,64,64]{3,0,2,1:T(8,128)} fusion(f32[7,32,64,64]{3,2,1,0:T(8,128)S(1)} %bitcast.785), kind=kOutput, calls=%fused_computation.9 | convolution fusion | flops 352335872 | bytes 7340032 | tf_op jit(solution)/shard_map/banm,ak->bknm/dot_general | solution.py:88
  324.3 15.1 %fusion.8 = f32[32,7,64,64]{3,0,2,1:T(8,128)} fusion(f32[7,32,64,64]{3,2,1,0:T(8,128)S(1)} %bitcast.786), kind=kOutput, calls=%fused_computation.11 | convolution fusion | flops 352335872 | bytes 7340032 | tf_op jit(solution)/shard_map/banm,ak->bknm/dot_general | solution.py:88
  339.5 22.3 %subtract_bitcast_fusion = (f32[7,32,64,64]{3,1,2,0:T(8,128)}, f32[7,32,64,64]{3,1,2,0:T(8,128)}) fusion(f32[32,64]{0,1:T(8,128)S(1)} %copy.677, f32[32,64]{0,1:T(8,128)S(1)} %copy.674, f32[32,7,64,64]{3,0,2,1:T(8,128)} %fusion.8, f32[32,7,64,64]{3,0,2,1:T(8,128)} %fusion.4, f32[32,7,64,64]{3,0,2,1:T(8,128)} %fusion.6, f32[7,32,64,64]{3,2,1,0:T(8,128)S(1)} %bitcast.787), kind=kOutput, calls=%fused_computation.6 | convolution fusion | flops 359675904 | bytes 22036480 | tf_op jit(solution)/shard_map/banm,ak->bknm/dot_general | solution.py:88
  361.8 12.5 %fusion = f32[64,7,32,64]{3,0,2,1:T(8,128)S(1)} fusion(f32[7,32,64,64]{3,1,2,0:T(8,128)} %get-tuple-element.33), kind=kOutput, calls=%fused_computation | convolution fusion | flops 704700416 | bytes 7340032 | tf_op jit(solution)/shard_map/bknm,nq->bmqk/dot_general | solution.py:88
  374.3 11.4 multiply_bitcast_fusion
  390.3 12.8 %copy.1009 = f32[7,64,2048]{1,0,2:T(8,128)} copy(f32[7,64,2048]{1,2,0:T(8,128)S(1)} %bitcast.794) | data formatting | bytes 7340032 | tf_op jit(solution)/shard_map/div | solution.py:216
  411.3 88.3 %all_to_all.288 = f32[4,1,229376]{2,1,0:T(1,128)} all-to-all(f32[4,1,229376]{2,1,0:T(1,128)} %reshape.1239), channel_id=1, replica_groups=mesh['row'=8,'col'=4] {'col'}, dimensions={0} | all-to-all | bytes 7340032 | tf_op jit(solution)/shard_map/all_to_all | solution.py:217
  499.6 13.7 %reduce.32 = f32[4,229376]{1,0:T(4,128)} reduce(f32[4,1,229376]{2,1,0:T(1,128)} %all_to_all.288, f32[]{:T(128)} %broadcast.1607), dimensions={1}, to_apply=%all_to_all.227.reduce_sub_computation | reduce | bytes 7340036 | tf_op jit(solution)/shard_map/all_to_all | solution.py:217
  538.0 15.4 %all-to-all-done.6 = f32[1,256,512]{2,0,1:T(1,128)S(1)} async-done(((f32[1,256,512]{2,0,1:T(1,128)}), f32[1,256,512]{2,0,1:T(1,128)S(1)}, u32[]{:S(2)}, u32[]{:S(2)}) %all-to-all-start.6) | async-done | bytes 524320 | tf_op jit(solution)/shard_map/all_to_all | solution.py:194
  705.0 30.3 %all_to_all.289 = f32[4,1,65536]{2,1,0:T(1,128)} all-to-all(f32[4,1,65536]{2,1,0:T(1,128)S(1)} %reshape.1249), channel_id=1, replica_groups=mesh['row'=8,'col'=4] {'col'}, dimensions={0} | all-to-all | bytes 2097152 | tf_op jit(solution)/shard_map/all_to_all | solution.py:217
  747.7 17.4 %all_to_all.290 = f32[1,256,512]{2,0,1:T(1,128)S(1)} all-to-all(f32[1,256,512]{2,0,1:T(1,128)S(1)} %copy.728), channel_id=1, replica_groups=mesh['row'=8,'col'=4] {'col'}, dimensions={1} | all-to-all | bytes 1048576 | tf_op jit(solution)/shard_map/all_to_all | solution.py:194
  824.3 10.6 reduce.46
  916.7 34.8 %reshape_squeeze.7 = f32[128,2,256,2]{3,2,1,0:T(8,128)} reshape(f32[1,4,64,512]{3,2,1,0:T(8,128)S(1)} %copy-done.25) | data formatting | bytes 1048576 | tf_op jit(solution)/shard_map/reshape;squeeze | solution.py:38
  951.5 13.3 %reduce_sum.29 = f32[128,256]{1,0:T(8,128)S(1)} reduce(f32[128,2,256,2]{3,2,1,0:T(8,128)} %reshape_squeeze.7, f32[]{:T(128)} %constant.215.clone.1), dimensions={1,3}, to_apply=%region_2.3 | reduce | flops 98304 | bytes 655364 | tf_op jit(solution)/shard_map/reduce_sum | solution.py:38
  964.8 34.9 %reshape_squeeze.6 = f32[128,2,256,2]{3,2,1,0:T(8,128)} reshape(f32[1,4,64,512]{3,2,1,0:T(8,128)S(1)} %copy-done.24) | data formatting | bytes 1048576 | tf_op jit(solution)/shard_map/reshape;squeeze | solution.py:38
  999.7 13.3 %reduce_sum.28 = f32[128,256]{1,0:T(8,128)S(1)} reduce(f32[128,2,256,2]{3,2,1,0:T(8,128)} %reshape_squeeze.6, f32[]{:T(128)} %constant.215.clone.1), dimensions={1,3}, to_apply=%region_1.2 | reduce | flops 98304 | bytes 655364 | tf_op jit(solution)/shard_map/reduce_sum | solution.py:38
  1027.5 35.6 %reshape.1180 = f32[128,2,256,2]{3,2,1,0:T(8,128)} reshape(f32[256,512]{1,0:T(8,128)} %get-tuple-element.29) | data formatting | bytes 1048576 | tf_op jit(solution)/shard_map/reshape | solution.py:38
  1063.1 13.2 %reduce_sum.27 = f32[128,256]{1,0:T(8,128)S(1)} reduce(f32[128,2,256,2]{3,2,1,0:T(8,128)} %reshape.1180, f32[]{:T(128)} %constant.215.clone.1), dimensions={1,3}, to_apply=%region_0.1 | reduce | flops 98304 | bytes 655364 | tf_op jit(solution)/shard_map/reduce_sum | solution.py:38
  1114.3 12.8 %fusion.26 = f32[1,16,128,256]{3,2,1,0:T(8,128)} fusion(f32[49,1,256]{2,1,0:T(1,128)S(1)} %copy-done.32, f32[1,128,256]{2,1,0:T(8,128)S(1)} %multiply_bitcast_fusion.2, f32[48,128,256]{2,1,0:T(8,128)S(1)} %bitcast.781, f32[49,1,256]{2,1,0:T(1,128)S(1)} %copy-done.30, f32[49,130,1]{2,1,0:T(8,128)S(1)} %copy-done, f32[49,130,1]{2,1,0:T(8,128)S(1)} %copy-done.1, ...), kind=kLoop, calls=%fused_computation.37 | loop fusion | flops 27787264 | bytes 19419024 | tf_op jit(solution)/shard_map/stack | solution.py:84
  1127.2 11.0 fusion.37
  1138.2 11.5 fusion.31
  (414 shorter events, 649.2 us)
Async XLA Ops:
  5.4 32.1 %all-to-all-start = ((f32[2,256,512]{2,0,1:T(2,128)}), f32[2,256,512]{2,0,1:T(2,128)S(1)}, u32[]{:S(2)}, u32[]{:S(2)}) async-start(f32[2,256,512]{2,0,1:T(2,128)} %pad_maximum_fusion.27), calls=%async_computation | async-start | bytes 2097152 | tf_op jit(solution)/shard_map/all_to_all | solution.py:194
  11.7 29.6 %copy-start.49 = (f32[22]{0:T(128)}, f32[22]{0:T(128)S(1)}, u32[]{:S(2)}) copy-start(f32[22]{0:T(128)S(1)} %compare_convert_fusion) | copy-start | bytes 268
  78.2 22.6 %all-to-all-start.1 = ((f32[32,1,2816]{2,1,0:T(1,128)}), f32[32,1,2816]{2,1,0:T(1,128)S(1)}, u32[]{:S(2)}, u32[]{:S(2)}) async-start(f32[32,1,2816]{2,1,0:T(1,128)} %reshape.1231), calls=%async_computation.1 | async-start | bytes 720896 | tf_op jit(solution)/shard_map/all_to_all | solution.py:197
  100.8 17.3 %all-to-all-start.2 = ((f32[32,1,2816]{2,1,0:T(1,128)}), f32[32,1,2816]{2,1,0:T(1,128)S(1)}, u32[]{:S(2)}, u32[]{:S(2)}) async-start(f32[32,1,2816]{2,1,0:T(1,128)} %reshape.1233), calls=%async_computation.2 | async-start | bytes 720896 | tf_op jit(solution)/shard_map/all_to_all | solution.py:200
  200.5 33.4 %all-to-all-start.3 = ((f32[32,1,9856]{2,1,0:T(1,128)}), f32[32,1,9856]{2,1,0:T(1,128)}, u32[]{:S(2)}, u32[]{:S(2)}) async-start(f32[32,1,9856]{2,1,0:T(1,128)} %reshape.1235), calls=%async_computation.3 | async-start | bytes 2523136 | tf_op jit(solution)/shard_map/all_to_all | solution.py:212
  233.9 34.2 %all-to-all-start.4 = ((f32[32,1,9856]{2,1,0:T(1,128)}), f32[32,1,9856]{2,1,0:T(1,128)}, u32[]{:S(2)}, u32[]{:S(2)}) async-start(f32[32,1,9856]{2,1,0:T(1,128)} %reshape.1237), calls=%async_computation.4 | async-start | bytes 2523136 | tf_op jit(solution)/shard_map/all_to_all | solution.py:213
  239.0 100.5 %copy-start.47 = (f32[32,64]{0,1:T(8,128)}, f32[32,64]{0,1:T(8,128)S(1)}, u32[]{:S(2)}) copy-start(f32[32,64]{0,1:T(8,128)S(1)} %copy.677) | copy-start | bytes 24580
  532.7 20.9 %copy-start.19 = (f32[1,4,64,512]{3,2,1,0:T(8,128)}, f32[1,4,64,512]{3,2,1,0:T(8,128)S(1)}, u32[]{:S(2)}) copy-start(f32[1,4,64,512]{3,2,1,0:T(8,128)S(1)} %get-tuple-element.55) | copy-start | bytes 1572868
  534.2 19.2 %all-to-all-start.6 = ((f32[1,256,512]{2,0,1:T(1,128)}), f32[1,256,512]{2,0,1:T(1,128)S(1)}, u32[]{:S(2)}, u32[]{:S(2)}) async-start(f32[1,256,512]{2,0,1:T(1,128)} %copy.684), calls=%async_computation.6 | async-start | bytes 1048576 | tf_op jit(solution)/shard_map/all_to_all | solution.py:194
  568.7 15.4 %all-to-all-start.7 = ((f32[32,1,1408]{2,1,0:T(1,128)}), f32[32,1,1408]{2,1,0:T(1,128)S(1)}, u32[]{:S(2)}, u32[]{:S(2)}) async-start(f32[32,1,1408]{2,1,0:T(1,128)} %reshape.1241), calls=%async_computation.7 | async-start | bytes 360448 | tf_op jit(solution)/shard_map/all_to_all | solution.py:197
  584.1 15.2 %all-to-all-start.8 = ((f32[32,1,1408]{2,1,0:T(1,128)}), f32[32,1,1408]{2,1,0:T(1,128)S(1)}, u32[]{:S(2)}, u32[]{:S(2)}) async-start(f32[32,1,1408]{2,1,0:T(1,128)} %reshape.1243), calls=%async_computation.8 | async-start | bytes 360448 | tf_op jit(solution)/shard_map/all_to_all | solution.py:200
  620.4 14.2 %all-to-all-start.10 = ((f32[32,1,2816]{2,1,0:T(1,128)}), f32[32,1,2816]{2,1,0:T(1,128)S(1)}, u32[]{:S(2)}, u32[]{:S(2)}) async-start(f32[32,1,2816]{2,1,0:T(1,128)} %reshape.1245), calls=%async_computation.10 | async-start | bytes 720896 | tf_op jit(solution)/shard_map/all_to_all | solution.py:213
  634.6 17.7 %all-to-all-start.9 = ((f32[32,1,2816]{2,1,0:T(1,128)}), f32[32,1,2816]{2,1,0:T(1,128)S(1)}, u32[]{:S(2)}, u32[]{:S(2)}) async-start(f32[32,1,2816]{2,1,0:T(1,128)} %reshape.1247), calls=%async_computation.9 | async-start | bytes 720896 | tf_op jit(solution)/shard_map/all_to_all | solution.py:212
  780.5 14.1 %all-to-all-start.13 = ((f32[32,1,1408]{2,1,0:T(1,128)}), f32[32,1,1408]{2,1,0:T(1,128)S(1)}, u32[]{:S(2)}, u32[]{:S(2)}) async-start(f32[32,1,1408]{2,1,0:T(1,128)} %reshape.1251), calls=%async_computation.13 | async-start | bytes 360448 | tf_op jit(solution)/shard_map/all_to_all | solution.py:197
  794.6 15.4 %all-to-all-start.14 = ((f32[32,1,1408]{2,1,0:T(1,128)}), f32[32,1,1408]{2,1,0:T(1,128)S(1)}, u32[]{:S(2)}, u32[]{:S(2)}) async-start(f32[32,1,1408]{2,1,0:T(1,128)} %reshape.1253), calls=%async_computation.14 | async-start | bytes 360448 | tf_op jit(solution)/shard_map/all_to_all | solution.py:200
  836.6 17.6 %all-to-all-start.15 = ((f32[32,1,1408]{2,1,0:T(1,128)}), f32[32,1,1408]{2,1,0:T(1,128)S(1)}, u32[]{:S(2)}, u32[]{:S(2)}) async-start(f32[32,1,1408]{2,1,0:T(1,128)} %reshape.1255), calls=%async_computation.15 | async-start | bytes 360448 | tf_op jit(solution)/shard_map/all_to_all | solution.py:212
  854.2 15.1 %all-to-all-start.16 = ((f32[32,1,1408]{2,1,0:T(1,128)}), f32[32,1,1408]{2,1,0:T(1,128)S(1)}, u32[]{:S(2)}, u32[]{:S(2)}) async-start(f32[32,1,1408]{2,1,0:T(1,128)} %reshape.1257), calls=%async_computation.16 | async-start | bytes 360448 | tf_op jit(solution)/shard_map/all_to_all | solution.py:213
  904.2 110.5 %all-to-all-start.17 = ((f32[4,1,32768]{2,1,0:T(1,128)}), f32[4,1,32768]{2,1,0:T(1,128)S(1)}, u32[]{:S(2)}, u32[]{:S(2)}) async-start(f32[4,1,32768]{2,1,0:T(1,128)} %reshape.1259), calls=%async_computation.17 | async-start | bytes 1048576 | tf_op jit(solution)/shard_map/all_to_all | solution.py:217
  951.5 13.3 %copy-start.24 = (f32[1,4,64,512]{3,2,1,0:T(8,128)S(1)}, f32[1,4,64,512]{3,2,1,0:T(8,128)}, u32[]{:S(2)}) copy-start(f32[1,4,64,512]{3,2,1,0:T(8,128)} %get-tuple-element.51) | copy-start | bytes 1572868
  999.7 14.0 %copy-start.26 = (f32[1,4,64,512]{3,1,2,0:T(4,128)S(1)}, f32[1,4,64,512]{3,1,2,0:T(4,128)}, u32[]{:S(2)}) copy-start(f32[1,4,64,512]{3,1,2,0:T(4,128)} %get-tuple-element.66) | copy-start | bytes 1572868
  1077.6 4.7 collective-permute-start
  1077.7 4.6 collective-permute-start.1
  1093.9 9.3 collective-permute-start.2
  1100.7 6.1 collective-permute-start.3
  (49 other events, 255.9 us)
where the time goes:
time: 1160 us
  local copies, waits for them, and re-layouts  392 us (34%)
  matrix products  270 us (23%)
  other arithmetic  200 us (17%)
  blocking collectives  136 us (12%)
  waiting for transfers between devices  80.1 us (7%)
  starting transfers between devices  75.2 us (6%)
    dot_general x84, matrix products, product(): return jnp.einsum(form, left, right, precision=lax.Precision.HIGHEST)  270 us
    all_to_all x2, blocking collectives, inverse(): lax.all_to_all(pencil, 'col', split_axis=2, concat_axis=1, tiled=True)  119 us
    unnamed x150, local copies, waits for them, and re-layouts  111 us
    another operation x2, local copies, waits for them, and re-layouts, coarsen(): return source.reshape(rows_out, COARSE, cols_out, COARSE).mean(axis=(1, 3))  69.7 us
    another operation x4, other arithmetic, flow_update(): return jnp.stack([next_u, next_v, next_w])  41.6 us
    all_to_all x2, waiting for transfers between devices, forward(): lax.all_to_all(stacked, 'col', split_axis=1, concat_axis=2, tiled=True)  40.8 us
    reduce_sum x3, other arithmetic, coarsen(): return source.reshape(rows_out, COARSE, cols_out, COARSE).mean(axis=(1, 3))  39.8 us
    unnamed x8, other arithmetic  37.8 us
  transfers between devices with their start and end apart: 19, of which 11 were waited for; matrix products, arithmetic and copies ran while one was open for 22% of the time, Pallas kernels for 0%

commit v1 on v0

--- a/solution.py
+++ b/solution.py
@@ -11,6 +11,12 @@
 FLOW_STEP = 0.5
 VISCOSITY = 0.2
 DECAY_RATE = 0.05
+
+
+def trade_parts(x, axis, split, join):
+    shards = jnp.split(x, lax.axis_size(axis), axis=split)
+    received = lax.all_to_all(jnp.stack(shards), axis, 0, 0)
+    return jnp.concatenate(received, axis=join)
 
 
 def with_halo(x, sides, width):
@@ -214,7 +220,7 @@
         )
         full_real, full_imag = unfold_half(full_real, full_imag, kept_modes)
         pencil = transform(full_real, full_imag, 1.0, "back", True) / float(NX * NY)
-        return lax.all_to_all(pencil, "col", split_axis=2, concat_axis=1, tiled=True)
+        return trade_parts(pencil, "col", 2, 1)
 
     first_real, first_imag = forward(jnp.stack([surface_potential, surface_height]))
     pot_hat = (first_real[0], first_imag[0])

time: 1160 us -> 1080 us (0.931)
  local copies, waits for them, and re-layouts: 392 us -> 338 us
  other arithmetic: 200 us -> 171 us
    unnamed x150 -> x142, local copies, waits for them, and re-layouts: 111 us -> 82 us
    div x5 -> x3, local copies, waits for them, and re-layouts: 28.7 us -> 6.14 us  [inverse(): pencil = transform(full_real, full_imag, 1.0, 'back', True) / float(NX * NY)]
    all_to_all x3 -> x0, other arithmetic: 21.3 us -> none  [inverse(): lax.all_to_all(pencil, 'col', split_axis=2, concat_axis=1, tiled=True)]
    all_to_all x4 -> x2, local copies, waits for them, and re-layouts: 12.9 us -> 0.67 us  [trade_parts(): received = lax.all_to_all(jnp.stack(shards), axis, 0, 0)]
    unnamed x8 -> x7, other arithmetic: 37.8 us -> 27 us
  transfers between devices with their start and end apart: 19 -> 19, of which waited for: 11 -> 11; matrix products, arithmetic and copies ran while one was open for 22% -> 24% of each run, Pallas kernels for 0% -> 0%
where the time goes in v1:
time: 1080 us; the launch traced here: 1070 us
  local copies, waits for them, and re-layouts  338 us (31%)
  matrix products  270 us (25%)
  other arithmetic  171 us (16%)
  blocking collectives  134 us (12%)
  waiting for transfers between devices  79.7 us (7%)
  starting transfers between devices  75.7 us (7%)
    dot_general x84, matrix products, product(): return jnp.einsum(form, left, right, precision=lax.Precision.HIGHEST)  270 us
    all_to_all x2, blocking collectives, trade_parts(): received = lax.all_to_all(jnp.stack(shards), axis, 0, 0)  117 us
    unnamed x142, local copies, waits for them, and re-layouts  82 us
    another operation x2, local copies, waits for them, and re-layouts, coarsen(): return source.reshape(rows_out, COARSE, cols_out, COARSE).mean(axis=(1, 3))  69.6 us
    another operation x4, other arithmetic, flow_update(): return jnp.stack([next_u, next_v, next_w])  41.6 us
    all_to_all x2, waiting for transfers between devices, forward(): lax.all_to_all(stacked, 'col', split_axis=1, concat_axis=2, tiled=True)  40.3 us
    reduce_sum x3, other arithmetic, coarsen(): return source.reshape(rows_out, COARSE, cols_out, COARSE).mean(axis=(1, 3))  39.9 us
    reshape x1, local copies, waits for them, and re-layouts, coarsen(): return source.reshape(rows_out, COARSE, cols_out, COARSE).mean(axis=(1, 3))  35.6 us
  transfers between devices with their start and end apart: 19, of which 11 were waited for; matrix products, arithmetic and copies ran while one was open for 24% of the time, Pallas kernels for 0%

profile of v1, /device:TPU:0, one launch (start us, length us, event | category | flops | bytes accessed | tf_op | source)
XLA Modules:
  0.0 1070.5 jit_solution(11088245342983798772)
XLA Ops:
  12.0 25.5 %all-to-all-done = f32[2,256,512]{2,0,1:T(2,128)S(1)} async-done(((f32[2,256,512]{2,0,1:T(2,128)}), f32[2,256,512]{2,0,1:T(2,128)S(1)}, u32[]{:S(2)}, u32[]{:S(2)}) %all-to-all-start) | async-done | bytes 1048608 | tf_op jit(solution)/shard_map/all_to_all | solution.py:200
  54.0 18.9 %subtract_bitcast_fusion.3 = f32[2,64,32,64]{3,1,2,0:T(8,128)S(1)} fusion(f32[64,2,64,32]{2,0,3,1:T(8,128)S(1)} %fusion.71, f32[2,64,32,64]{3,2,1,0:T(8,128)S(1)} %get-tuple-element.53), kind=kOutput, calls=%fused_computation.120 | convolution fusion | flops 201646080 | bytes 3145728 | tf_op jit(solution)/shard_map/bmkn,nq->bqkm/dot_general | solution.py:94
  259.0 9.2 all-to-all-done.4
  294.1 14.8 %fusion.4 = f32[32,7,64,64]{3,0,2,1:T(8,128)} fusion(f32[7,32,64,64]{3,2,1,0:T(8,128)S(1)} %bitcast.796), kind=kOutput, calls=%fused_computation.8 | convolution fusion | flops 352335872 | bytes 7340032 | tf_op jit(solution)/shard_map/banm,ak->bknm/dot_general | solution.py:94
  308.9 14.8 %fusion.6 = f32[32,7,64,64]{3,0,2,1:T(8,128)} fusion(f32[7,32,64,64]{3,2,1,0:T(8,128)S(1)} %bitcast.797), kind=kOutput, calls=%fused_computation.10 | convolution fusion | flops 352335872 | bytes 7340032 | tf_op jit(solution)/shard_map/banm,ak->bknm/dot_general | solution.py:94
  324.3 15.1 %fusion.8 = f32[32,7,64,64]{3,0,2,1:T(8,128)} fusion(f32[7,32,64,64]{3,2,1,0:T(8,128)S(1)} %bitcast.798), kind=kOutput, calls=%fused_computation.12 | convolution fusion | flops 352335872 | bytes 7340032 | tf_op jit(solution)/shard_map/banm,ak->bknm/dot_general | solution.py:94
  339.4 22.3 %subtract_bitcast_fusion = (f32[7,32,64,64]{3,1,2,0:T(8,128)}, f32[7,32,64,64]{3,1,2,0:T(8,128)}) fusion(f32[32,64]{0,1:T(8,128)S(1)} %copy.510, f32[32,64]{0,1:T(8,128)S(1)} %copy.507, f32[32,7,64,64]{3,0,2,1:T(8,128)} %fusion.8, f32[32,7,64,64]{3,0,2,1:T(8,128)} %fusion.4, f32[32,7,64,64]{3,0,2,1:T(8,128)} %fusion.6, f32[7,32,64,64]{3,2,1,0:T(8,128)S(1)} %bitcast.799), kind=kOutput, calls=%fused_computation.7 | convolution fusion | flops 359675904 | bytes 22036480 | tf_op jit(solution)/shard_map/banm,ak->bknm/dot_general | solution.py:94
  361.7 12.7 %fusion = f32[64,7,32,64]{3,0,2,1:T(8,128)S(1)} fusion(f32[7,32,64,64]{3,1,2,0:T(8,128)} %get-tuple-element.33), kind=kOutput, calls=%fused_computation.1 | convolution fusion | flops 704700416 | bytes 7340032 | tf_op jit(solution)/shard_map/bknm,nq->bmqk/dot_general | solution.py:94
  374.3 11.4 %multiply_bitcast_fusion = f32[7,64,64,32]{1,2,3,0:T(8,128)S(1)} fusion(f32[64,7,32,64]{3,0,2,1:T(8,128)S(1)} %fusion, f32[7,32,64,64]{3,1,2,0:T(8,128)S(1)} %copy-done.4), kind=kOutput, calls=%fused_computation.5 | convolution fusion | flops 706535424 | bytes 11010048 | tf_op jit(solution)/shard_map/bknm,nq->bmqk/dot_general | solution.py:94
  400.5 87.8 %all_to_all.258 = f32[4,7,64,512]{3,2,1,0:T(8,128)S(1)} all-to-all(f32[4,7,64,512]{3,2,1,0:T(8,128)} %copy.514), channel_id=1, replica_groups=mesh['row'=8,'col'=4] {'col'}, dimensions={0} | all-to-all | bytes 7340032 | tf_op jit(solution)/shard_map/all_to_all | solution.py:18
  495.8 14.8 %all-to-all-done.6 = f32[1,256,512]{2,0,1:T(1,128)S(1)} async-done(((f32[1,256,512]{2,0,1:T(1,128)}), f32[1,256,512]{2,0,1:T(1,128)S(1)}, u32[]{:S(2)}, u32[]{:S(2)}) %all-to-all-start.6) | async-done | bytes 524320 | tf_op jit(solution)/shard_map/all_to_all | solution.py:200
  652.7 29.6 %all_to_all.259 = f32[4,2,64,512]{3,2,1,0:T(8,128)S(1)} all-to-all(f32[4,2,64,512]{3,2,1,0:T(8,128)S(1)} %copy.557), channel_id=1, replica_groups=mesh['row'=8,'col'=4] {'col'}, dimensions={0} | all-to-all | bytes 2097152 | tf_op jit(solution)/shard_map/all_to_all | solution.py:18
  684.1 16.6 %all_to_all.260 = f32[1,256,512]{2,0,1:T(1,128)S(1)} all-to-all(f32[1,256,512]{2,0,1:T(1,128)S(1)} %copy.559), channel_id=1, replica_groups=mesh['row'=8,'col'=4] {'col'}, dimensions={1} | all-to-all | bytes 1048576 | tf_op jit(solution)/shard_map/all_to_all | solution.py:200
  760.4 10.6 reduce.44
  778.2 10.4 reduce.42
  841.8 34.8 %reshape_squeeze.7 = f32[128,2,256,2]{3,2,1,0:T(8,128)} reshape(f32[1,4,64,512]{3,2,1,0:T(8,128)S(1)} %copy-done.25) | data formatting | bytes 1048576 | tf_op jit(solution)/shard_map/reshape;squeeze | solution.py:44
  876.6 13.3 %reduce_sum.29 = f32[128,256]{1,0:T(8,128)S(1)} reduce(f32[128,2,256,2]{3,2,1,0:T(8,128)} %reshape_squeeze.7, f32[]{:T(128)} %constant.215.clone.1), dimensions={1,3}, to_apply=%region_2.3 | reduce | flops 98304 | bytes 655364 | tf_op jit(solution)/shard_map/reduce_sum | solution.py:44
  889.9 34.8 %reshape_squeeze.6 = f32[128,2,256,2]{3,2,1,0:T(8,128)} reshape(f32[1,4,64,512]{3,2,1,0:T(8,128)S(1)} %copy-done.24) | data formatting | bytes 1048576 | tf_op jit(solution)/shard_map/reshape;squeeze | solution.py:44
  924.7 13.3 %reduce_sum.28 = f32[128,256]{1,0:T(8,128)S(1)} reduce(f32[128,2,256,2]{3,2,1,0:T(8,128)} %reshape_squeeze.6, f32[]{:T(128)} %constant.215.clone.1), dimensions={1,3}, to_apply=%region_1.2 | reduce | flops 98304 | bytes 655364 | tf_op jit(solution)/shard_map/reduce_sum | solution.py:44
  942.0 35.6 %reshape.1189 = f32[128,2,256,2]{3,2,1,0:T(8,128)} reshape(f32[256,512]{1,0:T(8,128)} %get-tuple-element.29) | data formatting | bytes 1048576 | tf_op jit(solution)/shard_map/reshape | solution.py:44
  977.5 13.2 %reduce_sum.27 = f32[128,256]{1,0:T(8,128)S(1)} reduce(f32[128,2,256,2]{3,2,1,0:T(8,128)} %reshape.1189, f32[]{:T(128)} %constant.215.clone.1), dimensions={1,3}, to_apply=%region_0.1 | reduce | flops 98304 | bytes 655364 | tf_op jit(solution)/shard_map/reduce_sum | solution.py:44
  1028.6 12.8 %fusion.26 = f32[1,16,128,256]{3,2,1,0:T(8,128)} fusion(f32[49,1,256]{2,1,0:T(1,128)S(1)} %copy-done.31, f32[1,128,256]{2,1,0:T(8,128)S(1)} %multiply_bitcast_fusion.2, f32[48,128,256]{2,1,0:T(8,128)S(1)} %bitcast.793, f32[49,1,256]{2,1,0:T(1,128)S(1)} %copy-done.29, f32[49,130,1]{2,1,0:T(8,128)S(1)} %copy-done, f32[49,130,1]{2,1,0:T(8,128)S(1)} %copy-done.1, ...), kind=kLoop, calls=%fused_computation.39 | loop fusion | flops 27787264 | bytes 19419024 | tf_op jit(solution)/shard_map/stack | solution.py:90
  1041.5 11.0 %fusion.37 = f32[1,16,128,256]{3,2,1,0:T(8,128)} fusion(f32[49,1,256]{2,1,0:T(1,128)S(1)} %copy-done.31, f32[1,128,256]{2,1,0:T(8,128)S(1)} %multiply_bitcast_fusion.2, f32[48,128,256]{2,1,0:T(8,128)S(1)} %bitcast.794, f32[49,1,256]{2,1,0:T(1,128)S(1)} %copy-done.29, f32[3,16,128,256]{3,2,1,0:T(8,128)S(1)} %bitcast.792, f32[1,128,256]{2,1,0:T(8,128)S(1)} %copy-done.37, ...), kind=kLoop, calls=%fused_computation.50 | loop fusion | flops 26214400 | bytes 19419024 | tf_op jit(solution)/shard_map/stack | solution.py:90
  1052.5 11.5 %fusion.31 = f32[1,16,128,256]{3,2,1,0:T(8,128)} fusion(f32[1,128,256]{2,1,0:T(8,128)S(1)} %copy-done.45, f32[15,128,256]{2,1,0:T(8,128)} %get-tuple-element.43, f32[15,128,256]{2,1,0:T(8,128)} %get-tuple-element.44, f32[49,1,256]{2,1,0:T(1,128)S(1)} %copy-done.31, f32[1,128,256]{2,1,0:T(8,128)S(1)} %multiply_bitcast_fusion.2, ...), kind=kLoop, calls=%fused_computation.44 | loop fusion | flops 27262976 | bytes 27676496 | tf_op jit(solution)/shard_map/stack | solution.py:90
  (405 shorter events, 572.8 us)
Async XLA Ops:
  5.4 32.1 %all-to-all-start = ((f32[2,256,512]{2,0,1:T(2,128)}), f32[2,256,512]{2,0,1:T(2,128)S(1)}, u32[]{:S(2)}, u32[]{:S(2)}) async-start(f32[2,256,512]{2,0,1:T(2,128)} %pad_maximum_fusion.29), calls=%async_computation | async-start | bytes 2097152 | tf_op jit(solution)/shard_map/all_to_all | solution.py:200
  11.7 29.6 %copy-start.48 = (f32[22]{0:T(128)}, f32[22]{0:T(128)S(1)}, u32[]{:S(2)}) copy-start(f32[22]{0:T(128)S(1)} %compare_convert_fusion) | copy-start | bytes 268
  78.2 22.6 %all-to-all-start.1 = ((f32[32,1,2816]{2,1,0:T(1,128)}), f32[32,1,2816]{2,1,0:T(1,128)S(1)}, u32[]{:S(2)}, u32[]{:S(2)}) async-start(f32[32,1,2816]{2,1,0:T(1,128)} %reshape.1240), calls=%async_computation.1 | async-start | bytes 720896 | tf_op jit(solution)/shard_map/all_to_all | solution.py:203
  100.8 17.3 %all-to-all-start.2 = ((f32[32,1,2816]{2,1,0:T(1,128)}), f32[32,1,2816]{2,1,0:T(1,128)S(1)}, u32[]{:S(2)}, u32[]{:S(2)}) async-start(f32[32,1,2816]{2,1,0:T(1,128)} %reshape.1242), calls=%async_computation.2 | async-start | bytes 720896 | tf_op jit(solution)/shard_map/all_to_all | solution.py:206
  200.6 33.4 %all-to-all-start.3 = ((f32[32,1,9856]{2,1,0:T(1,128)}), f32[32,1,9856]{2,1,0:T(1,128)}, u32[]{:S(2)}, u32[]{:S(2)}) async-start(f32[32,1,9856]{2,1,0:T(1,128)} %reshape.1244), calls=%async_computation.3 | async-start | bytes 2523136 | tf_op jit(solution)/shard_map/all_to_all | solution.py:218
  234.0 34.2 %all-to-all-start.4 = ((f32[32,1,9856]{2,1,0:T(1,128)}), f32[32,1,9856]{2,1,0:T(1,128)}, u32[]{:S(2)}, u32[]{:S(2)}) async-start(f32[32,1,9856]{2,1,0:T(1,128)} %reshape.1246), calls=%async_computation.4 | async-start | bytes 2523136 | tf_op jit(solution)/shard_map/all_to_all | solution.py:219
  239.1 100.3 %copy-start.46 = (f32[32,64]{0,1:T(8,128)}, f32[32,64]{0,1:T(8,128)S(1)}, u32[]{:S(2)}) copy-start(f32[32,64]{0,1:T(8,128)S(1)} %copy.510) | copy-start | bytes 24580
  490.8 20.1 %copy-start.19 = (f32[1,4,64,512]{3,2,1,0:T(8,128)}, f32[1,4,64,512]{3,2,1,0:T(8,128)S(1)}, u32[]{:S(2)}) copy-start(f32[1,4,64,512]{3,2,1,0:T(8,128)S(1)} %get-tuple-element.59) | copy-start | bytes 1572868
  492.3 18.3 %all-to-all-start.6 = ((f32[1,256,512]{2,0,1:T(1,128)}), f32[1,256,512]{2,0,1:T(1,128)S(1)}, u32[]{:S(2)}, u32[]{:S(2)}) async-start(f32[1,256,512]{2,0,1:T(1,128)} %copy.516), calls=%async_computation.6 | async-start | bytes 1048576 | tf_op jit(solution)/shard_map/all_to_all | solution.py:200
  526.0 14.4 %all-to-all-start.7 = ((f32[32,1,1408]{2,1,0:T(1,128)}), f32[32,1,1408]{2,1,0:T(1,128)S(1)}, u32[]{:S(2)}, u32[]{:S(2)}) async-start(f32[32,1,1408]{2,1,0:T(1,128)} %reshape.1248), calls=%async_computation.7 | async-start | bytes 360448 | tf_op jit(solution)/shard_map/all_to_all | solution.py:203
  540.4 15.4 %all-to-all-start.8 = ((f32[32,1,1408]{2,1,0:T(1,128)}), f32[32,1,1408]{2,1,0:T(1,128)S(1)}, u32[]{:S(2)}, u32[]{:S(2)}) async-start(f32[32,1,1408]{2,1,0:T(1,128)} %reshape.1250), calls=%async_computation.8 | async-start | bytes 360448 | tf_op jit(solution)/shard_map/all_to_all | solution.py:206
  576.9 14.2 %all-to-all-start.10 = ((f32[32,1,2816]{2,1,0:T(1,128)}), f32[32,1,2816]{2,1,0:T(1,128)S(1)}, u32[]{:S(2)}, u32[]{:S(2)}) async-start(f32[32,1,2816]{2,1,0:T(1,128)} %reshape.1252), calls=%async_computation.10 | async-start | bytes 720896 | tf_op jit(solution)/shard_map/all_to_all | solution.py:219
  591.0 17.5 %all-to-all-start.9 = ((f32[32,1,2816]{2,1,0:T(1,128)}), f32[32,1,2816]{2,1,0:T(1,128)S(1)}, u32[]{:S(2)}, u32[]{:S(2)}) async-start(f32[32,1,2816]{2,1,0:T(1,128)} %reshape.1254), calls=%async_computation.9 | async-start | bytes 720896 | tf_op jit(solution)/shard_map/all_to_all | solution.py:218
  716.1 14.9 %all-to-all-start.13 = ((f32[32,1,1408]{2,1,0:T(1,128)}), f32[32,1,1408]{2,1,0:T(1,128)S(1)}, u32[]{:S(2)}, u32[]{:S(2)}) async-start(f32[32,1,1408]{2,1,0:T(1,128)} %reshape.1256), calls=%async_computation.13 | async-start | bytes 360448 | tf_op jit(solution)/shard_map/all_to_all | solution.py:203
  731.0 15.2 %all-to-all-start.14 = ((f32[32,1,1408]{2,1,0:T(1,128)}), f32[32,1,1408]{2,1,0:T(1,128)S(1)}, u32[]{:S(2)}, u32[]{:S(2)}) async-start(f32[32,1,1408]{2,1,0:T(1,128)} %reshape.1258), calls=%async_computation.14 | async-start | bytes 360448 | tf_op jit(solution)/shard_map/all_to_all | solution.py:206
  772.6 17.6 %all-to-all-start.15 = ((f32[32,1,1408]{2,1,0:T(1,128)}), f32[32,1,1408]{2,1,0:T(1,128)S(1)}, u32[]{:S(2)}, u32[]{:S(2)}) async-start(f32[32,1,1408]{2,1,0:T(1,128)} %reshape.1260), calls=%async_computation.15 | async-start | bytes 360448 | tf_op jit(solution)/shard_map/all_to_all | solution.py:218
  790.2 15.3 %all-to-all-start.16 = ((f32[32,1,1408]{2,1,0:T(1,128)}), f32[32,1,1408]{2,1,0:T(1,128)S(1)}, u32[]{:S(2)}, u32[]{:S(2)}) async-start(f32[32,1,1408]{2,1,0:T(1,128)} %reshape.1262), calls=%async_computation.16 | async-start | bytes 360448 | tf_op jit(solution)/shard_map/all_to_all | solution.py:219
  828.4 110.4 %all-to-all-start.17 = ((f32[4,1,64,512]{3,2,1,0:T(8,128)}), f32[4,1,64,512]{3,2,1,0:T(8,128)}, u32[]{:S(2)}, u32[]{:S(2)}) async-start(f32[4,1,64,512]{3,2,1,0:T(8,128)} %copy.600), calls=%async_computation.17 | async-start | bytes 1048576 | tf_op jit(solution)/shard_map/all_to_all | solution.py:18
  924.7 14.1 %copy-start.20 = (f32[1,4,64,512]{3,2,1,0:T(8,128)S(1)}, f32[1,4,64,512]{3,2,1,0:T(8,128)}, u32[]{:S(2)}) copy-start(f32[1,4,64,512]{3,2,1,0:T(8,128)} %copy-done.19) | copy-start | bytes 1572868
  924.7 14.1 %copy-start.22 = (f32[1,4,64,512]{3,2,1,0:T(8,128)S(1)}, f32[1,4,64,512]{3,2,1,0:T(8,128)}, u32[]{:S(2)}) copy-start(f32[1,4,64,512]{3,2,1,0:T(8,128)} %get-tuple-element.58) | copy-start | bytes 1572868
  992.0 4.8 collective-permute-start
  992.1 4.7 collective-permute-start.1
  1008.2 9.4 collective-permute-start.2
  1015.1 6.1 collective-permute-start.3
  (48 other events, 259.5 us)
